TPU v7x, 32 devices: a whole 2x2x4 slice. The times are simulated.
32 devices in a mesh: gz: 8 (over z, x), col: 4 (over y, core).
Axes of the slice: x: 2, y: 2, z: 4, core: 2. Of those that a mesh axis runs over, the one named last changes fastest.
Arguments:
- source: float32 [512, 2048], P('gz', 'col'), may hold values from -6 to 6
- z_vectors: float32 [512, 512], P('gz', 'col'), may hold values from -0.375 to 0.375
- x_vectors: float32 [4, 4], replicated, may hold values from -3 to 3
- y_vectors: float32 [512, 512], replicated, may hold values from -0.25 to 0.25
- z_values: float32 [512], replicated, may hold values from 0.1 to 3
- x_values: float32 [4], replicated, may hold values from 0.1 to 3
- y_values: float32 [512], replicated, may hold values from 0.1 to 3
Outputs:
- solution: float32 [512, 2048], P('gz', 'col')
All inputs are finite; a program needn't handle non-finite values.
Results may differ from a plain program's by a relative error of at most 0.000092.
Values sent between devices are 32-bit elements; how exact they have to be, the bound alone decides.
A program may use at most 64 MiB of HBM per device.

v0:
```python
import functools

import jax
import jax.numpy as jnp
from jax import lax
from jax.experimental import pallas as pl
from jax.experimental.pallas import tpu as pltpu
from jax.sharding import PartitionSpec as P

f32, bf16 = jnp.float32, jnp.bfloat16
MESH = pl.DeviceIdType.MESH


def split(x):
    hi = x.astype(bf16)
    return hi, (x - hi.astype(f32)).astype(bf16)


def dot(a, b, flip):
    dims = (((1,), (1 if flip else 0,)), ((), ()))
    return lax.dot_general(a, b, dims, preferred_element_type=f32)


def product(a, b_hi, b_lo, flip=False):
    rows = a.shape[0]
    a_hi, a_lo = split(a)
    both = dot(jnp.concatenate([a_hi, a_lo], axis=0), b_hi, flip)
    return both[:rows] + (both[rows:] + dot(a_hi, b_lo, flip))


def each(count, body, start=0, down=False):
    if count <= 8:
        order = range(start, count)
        for step in reversed(order) if down else order:
            body(step)
    else:
        lax.fori_loop(
            start, count,
            lambda step, _: (body(count - 1 + start - step if down else step), 0)[1], 0,
        )


def flipped(index, count, d):
    total, unit = 0, 1
    while unit < count:
        total = total + unit * lax.rem(index // unit + d // unit, 2)
        unit *= 2
    return total


def kernel(
    n, m, pack, group,
    source, z_vectors, y_vectors, z_values, y_values, x_vectors, x_values,
    out,
    src, y_raw, y_hi, y_lo, zval, yval, y_col,
    inverse_sum, v, w_hi, w_lo, a_t, fields, partial, inner_in, half, outer_in, final, back,
    load_sem, send_sem, a_sem, v_sem, outer_sem, inner_sem, inner2_sem, r1_sem, r2_sem, q_sem,
):
    g, c = lax.axis_index("gz"), lax.axis_index("col")
    rows, width = src.shape
    lanes = pack * rows
    jr = a_t.shape[1]
    kc = v.shape[2]
    span = width // pack
    inner_bit = lax.rem(c, 2)
    outer_bit = c // 2
    inner = outer_bit * 2 + (1 - inner_bit)
    outer = (1 - outer_bit) * 2 + inner_bit
    across = (1 - outer_bit) * 2 + (1 - inner_bit)

    def at(peer_g, peer_c):
        return {"gz": peer_g, "col": peer_c}

    def send(src_ref, dst_ref, lane, recv, peer):
        pltpu.make_async_remote_copy(
            src_ref=src_ref, dst_ref=dst_ref, send_sem=send_sem.at[lane], recv_sem=recv,
            device_id=peer, device_id_type=MESH,
        ).start()

    def arrived(ref, sem):
        pltpu.make_async_copy(ref, ref, sem).wait()

    barrier = pltpu.get_barrier_semaphore()

    def greet(d):
        pl.semaphore_signal(
            barrier, inc=1, device_id=at(flipped(g, n, d), c), device_id_type=MESH
        )

    each(n, greet, 1, down=True)
    for peer in (outer, inner):
        pl.semaphore_signal(barrier, inc=1, device_id=at(g, peer), device_id_type=MESH)

    pl.semaphore_signal(barrier, inc=1, device_id=at(g, across), device_id_type=MESH)
    loads = [
        pltpu.make_async_copy(a, b, load_sem.at[i])
        for i, (a, b) in enumerate(
            [(z_vectors, v.at[0]), (y_vectors, y_raw), (source, src), (z_values, zval), (y_values, yval)]
        )
    ]
    for copy in loads:
        copy.start()
    loads[1].wait()
    hi, lo = split(y_raw[...])
    y_hi[...] = hi
    y_lo[...] = lo
    loads[2].wait()
    along = product(src[...], hi, lo)
    stacked = jnp.concatenate([along[:, h * span:(h + 1) * span] for h in range(pack)], axis=0)
    a_t[...] = jnp.transpose(stacked).reshape(n, jr, lanes)
    fields[c, 0] = a_t[g]
    loads[0].wait()
    pl.semaphore_wait(barrier, n + 2)

    def send_a(d):
        peer = flipped(g, n, d)
        send(a_t.at[peer], fields.at[c, d], 0, a_sem.at[d], at(peer, c))

    def send_v(held, d):
        send(v.at[held], v.at[held + d], 1, v_sem.at[held + d], at(flipped(g, n, d), c))

    def pass_v(held, unit):
        each(n // 2, lambda e: send_v(0, 2 * e), 1, down=True)
        send_v(0, 1)

    def relay_v(held):
        arrived(v.at[held], v_sem.at[held])
        send_v(held, 1)

    def relay(d, direct=False):
        block = fields.at[c, d]
        send(block, block, 2, outer_sem.at[d], at(g, outer))
        send(block, block, 3, inner_sem.at[d], at(g, inner))
        if direct:
            send(block, block, 4, inner2_sem.at[d], at(g, across))

    def relay_near(d):
        arrived(fields.at[c, d], a_sem.at[d])
        relay(d)

    def relay_far(d):
        arrived(fields.at[c, d], a_sem.at[d])
        relay(d, True)

    def relay_outer(d):
        block = fields.at[outer, d]
        arrived(block, outer_sem.at[d])
        send(block, block, 4, inner2_sem.at[d], at(g, inner))

    def build(d):
        hi, lo = split(v[d])
        for h in range(pack):
            w_hi[d, h * rows:(h + 1) * rows, h * kc:(h + 1) * kc] = hi
            w_lo[d, h * rows:(h + 1) * rows, h * kc:(h + 1) * kc] = lo

    near_count = n // 2
    pass_v(0, n // 2)
    each(n, send_a, 1, down=True)
    relay(0)

    if pack > 1:
        w_hi[...] = jnp.zeros_like(w_hi)
        w_lo[...] = jnp.zeros_like(w_lo)
    build(0)
    loads[3].wait()
    loads[4].wait()
    y_col[...] = jnp.transpose(jnp.broadcast_to(yval[...], (128, width)))
    z_part = zval[:, pl.ds(pl.multiple_of(c * kc, 128), kc)]
    base = jnp.concatenate(
        [
            z_part + y_col[pl.ds(pl.multiple_of(h * span + g * jr, 8), jr), 0:1]
            for h in range(pack)
        ],
        axis=1,
    )
    for i in range(m):
        inverse_sum[i] = 1.0 / (base + x_values[i])

    held, unit = [0], n // 2
    while unit > 1:
        held += [h + unit for h in held]
        unit //= 2
    queue = held[1:]
    if n <= 8:
        for d in range(1, n):
            (relay_near if d < near_count else relay_far)(d)
            if d > 1 and queue:
                relay_v(queue.pop(0))
    for h in queue:
        relay_v(h)
    if n > 8:
        each(near_count, relay_near, 1)
        each(n, relay_far, near_count)
    each(near_count, relay_outer)

    def ready(d):
        arrived(fields.at[inner, d], inner_sem.at[d])
        arrived(fields.at[across, d], inner2_sem.at[d])

    def ready_outer(d):
        arrived(fields.at[outer, d], outer_sem.at[d])

    def received(d):
        if d % 2:
            arrived(v.at[d], v_sem.at[d])
        if d:
            build(d)
        if d >= near_count:
            ready_outer(d)
        ready(d)

    if n > 8:
        each(n // 2, lambda e: build(2 * e), 1)

        def build_odd(e):
            arrived(v.at[2 * e + 1], v_sem.at[2 * e + 1])
            build(2 * e + 1)

        each(n // 2, build_odd)
        each(n, ready_outer, near_count)
        each(n, ready)

    def lhs(first):
        parts = [fields[:, first + s].reshape(m * jr, lanes) for s in range(group)]
        return parts[0] if group == 1 else jnp.concatenate(parts, axis=1)

    def weights(ref, first):
        return ref[pl.ds(first, group)].reshape(group * lanes, pack * kc)

    def term(s):
        if n <= 8:
            for k in range(group):
                received(s * group + k)
        return product(lhs(s * group), weights(w_hi, s * group), weights(w_lo, s * group))

    steps = n // group
    if steps <= 8:
        modes = term(0)
        for s in range(1, steps):
            modes = modes + term(s)
    else:
        modes = lax.fori_loop(1, steps, lambda s, acc: acc + term(s), term(0))

    lines = [modes[x * jr:(x + 1) * jr] for x in range(m)]
    scaled = []
    for i in range(m):
        total = x_vectors[0, i] * lines[0]
        for x in range(1, m):
            total = total + x_vectors[x, i] * lines[x]
        scaled.append(total * inverse_sum[i])
    turned = []
    for x in [o * 2 + b for b in range(2) for o in range(m // 2)]:
        total = x_vectors[x, 0] * scaled[0]
        for i in range(1, m):
            total = total + x_vectors[x, i] * scaled[i]
        turned.append(total)
    turned = jnp.concatenate(turned, axis=0)
    t_hi, t_lo = split(turned)
    t_both = jnp.concatenate([t_hi, t_lo], axis=0)

    def inverse(s):
        first = s * group
        wh, wl = weights(w_hi, first), weights(w_lo, first)
        both = dot(t_both, wh, True)
        values = both[:m * jr] + (both[m * jr:] + dot(t_hi, wl, True))
        for k in reversed(range(group)):
            partial[first + k] = values[:, k * lanes:(k + 1) * lanes].reshape(2, m // 2, jr, lanes)
        for k in reversed(range(group)):
            send(
                partial.at[first + k, 1 - inner_bit], inner_in.at[first + k], 5,
                r1_sem.at[first + k], at(g, inner),
            )

    each(steps, inverse, down=True)

    def fold_inner(d):
        arrived(inner_in.at[d], r1_sem.at[d])
        half[d] = partial[d, inner_bit] + inner_in[d]
        send(half.at[d, 1 - outer_bit], outer_in.at[d], 6, r2_sem.at[d], at(g, outer))

    each(n, fold_inner, down=True)

    def fold_outer(d):
        arrived(outer_in.at[d], r2_sem.at[d])
        final[d] = half[d, outer_bit] + outer_in[d]
        send(final.at[d], back.at[g], 7, q_sem.at[d], at(flipped(g, n, d), c))

    each(n, fold_outer, 1, down=True)
    arrived(outer_in.at[0], r2_sem.at[0])
    back[g] = half[0, outer_bit] + outer_in[0]

    each(n, lambda d: arrived(back.at[flipped(g, n, d)], q_sem.at[d]), 1, down=True)
    turned_back = jnp.transpose(back[...].reshape(n * jr, lanes))
    lines_back = jnp.concatenate(
        [turned_back[h * rows:(h + 1) * rows] for h in range(pack)], axis=1
    ) if pack > 1 else turned_back
    out[...] = product(lines_back, y_hi[...], y_lo[...], True)

    arrived(a_t.at[pl.ds(0, n - 1)], send_sem.at[0])
    arrived(v.at[pl.ds(0, n - 1)], send_sem.at[1])
    for lane in (2, 3, 4):
        arrived(fields.at[c], send_sem.at[lane])
    arrived(inner_in, send_sem.at[5])
    arrived(outer_in, send_sem.at[6])
    arrived(final.at[pl.ds(0, n - 1)], send_sem.at[7])


def shards(n, m, source, z_vectors, x_vectors, y_vectors, z_values, x_values, y_values):
    rows, width = source.shape
    kc = z_vectors.shape[1]
    pack = max(1, 128 // rows)
    while pack > 1 and width % (n * pack * 8):
        pack //= 2
    lanes, jr = pack * rows, width // (n * pack)
    group = 2 if lanes % 128 == 0 and n % 2 == 0 else 1
    vm = pltpu.VMEM
    dma = pltpu.SemaphoreType.DMA
    hbm, smem = pl.BlockSpec(memory_space=pl.ANY), pl.BlockSpec(memory_space=pltpu.SMEM)
    return pl.pallas_call(
        functools.partial(kernel, n, m, pack, group),
        out_shape=jax.ShapeDtypeStruct((rows, width), f32),
        in_specs=[hbm] * 5 + [smem] * 2,
        out_specs=pl.BlockSpec(memory_space=vm),
        scratch_shapes=[
            vm((rows, width), f32),
            vm(y_vectors.shape, f32),
            vm(y_vectors.shape, bf16),
            vm(y_vectors.shape, bf16),
            vm((1, z_values.shape[0]), f32),
            vm((1, width), f32),
            vm((width, 128), f32),
            vm((m, jr, pack * kc), f32),
            vm((n, rows, kc), f32),
            vm((n, lanes, pack * kc), bf16),
            vm((n, lanes, pack * kc), bf16),
            vm((n, jr, lanes), f32),
            vm((m, n, jr, lanes), f32),
            vm((n, 2, m // 2, jr, lanes), f32),
            vm((n, m // 2, jr, lanes), f32),
            vm((n, m // 2, jr, lanes), f32),
            vm((n, jr, lanes), f32),
            vm((n, jr, lanes), f32),
            vm((n, jr, lanes), f32),
            dma((5,)),
            dma((8,)),
        ] + [dma((n,))] * 8,
        compiler_params=pltpu.CompilerParams(
            collective_id=0, has_side_effects=True, vmem_limit_bytes=60 * 1024 * 1024
        ),
    )(
        source, z_vectors, y_vectors, z_values.reshape(1, -1), y_values.reshape(1, -1),
        x_vectors, x_values,
    )


def solution(mesh):
    placed = (P("gz", "col"), P("gz", "col"), P(), P(), P(), P(), P())
    sizes = (mesh.shape["gz"], mesh.shape["col"])
    return jax.shard_map(
        functools.partial(shards, *sizes),
        mesh=mesh, in_specs=placed, out_specs=P("gz", "col"), check_vma=False,
    )
```

profile of v0, /device:TPU:0, one launch (start us, length us, event | category | flops | bytes accessed | tf_op | source)
XLA Modules:
  0.0 29.6 jit_solution(11933966939230026675)
XLA Ops:
  0.0 28.0 %shard_map.73 = f32[64,512]{1,0:T(8,128)} custom-call(f32[64,512]{1,0:T(8,128)} %source.1, f32[64,128]{1,0:T(8,128)} %z_vectors.1, f32[512,512]{1,0:T(8,128)} %y_vectors.1, f32[1,512]{1,0:T(1,128)} %bitcast.2, f32[1,512]{1,0:T(1,128)} %bitcast.3, f32[4,4]{1,0:T(4,128)} %x_vectors.1, f32[4]{0:T(128)} %x_values.1), custom_call_target="tpu_custom_call" | custom-call | tf_op jit(solution)/shard_map/pallas_call | solution.py:319
  28.0 1.6 %copy.9 = f32[64,512]{1,0:T(8,128)} copy(f32[64,512]{1,0:T(8,128)} %shard_map.73) | data formatting | bytes 262144
where the time goes:
time: 29.8 us; the launch traced here: 29.6 us
  Pallas kernels  28 us (94%)
  local copies, waits for them, and re-layouts  1.57 us (5%)
    pallas_call x1, Pallas kernels, shards(): pl.pallas_call(functools.partial(kernel, n, m, pack, group), out_shape=ja...  28 us
    unnamed x1, local copies, waits for them, and re-layouts  1.57 us

commit v1 on v0

--- a/solution.py
+++ b/solution.py
@@ -353,10 +353,280 @@
     )
 
 
+def bits(index, count):
+    deltas, unit = [], 1
+    while unit < count:
+        deltas.append(unit * (1 - 2 * lax.rem(index // unit, 2)))
+        unit *= 2
+    return deltas
+
+
+def moved(index, deltas, d):
+    for place, delta in enumerate(deltas):
+        if d >> place & 1:
+            index = index + delta
+    return index
+
+
+def whole_kernel(
+    n, m,
+    source, z_vectors, y_vectors, z_values, y_values, x_vectors, x_values,
+    out,
+    src, y_raw, y_hi, y_lo, zval, yval, y_col,
+    inverse_sum, v, w_hi, w_lo, a_t, fields, partial, back,
+    load_sem, send_sem, a_sem, q_sem, line_sem, x_sem, y_sem, corner_sem, core_sem,
+):
+    g, c = lax.axis_index("gz"), lax.axis_index("col")
+    rows, width = src.shape
+    kc = v.shape[2]
+    jr, lanes = a_t.shape[1:]
+    span = width // 2
+    order = n * rows
+    half = rows // 2
+    g_bits, c_bits = bits(g, n), bits(c, m)
+    me = g * m + c
+
+    def at(d):
+        return {"gz": moved(g, g_bits, d // m), "col": moved(c, c_bits, d % m)}
+
+    def slot(d):
+        return moved(g, g_bits, d // m) * m + moved(c, c_bits, d % m)
+
+    def send(src_ref, dst_ref, lane, recv, peer):
+        pltpu.make_async_remote_copy(
+            src_ref=src_ref, dst_ref=dst_ref, send_sem=send_sem.at[lane], recv_sem=recv,
+            device_id=peer, device_id_type=MESH,
+        ).start()
+
+    def arrived(ref, sem):
+        pltpu.make_async_copy(ref, ref, sem).wait()
+
+    loads = [
+        pltpu.make_async_copy(a, b, load_sem.at[i])
+        for i, (a, b) in enumerate(
+            [(z_vectors, v.at[me]), (y_vectors, y_raw), (source, src), (z_values, zval), (y_values, yval)]
+        )
+    ]
+    for copy in loads:
+        copy.start()
+    barrier = pltpu.get_barrier_semaphore()
+    far = sorted(range(1, n * m), key=lambda d: -bin(d).count("1") - (d // m // 2))
+    for d in far:
+        pl.semaphore_signal(barrier, inc=1, device_id=at(d), device_id_type=MESH)
+
+    loads[1].wait()
+    hi, lo = split(y_raw[...])
+    y_hi[...] = hi
+    y_lo[...] = lo
+    loads[2].wait()
+    along = product(src[...], hi, lo)
+    stacked = jnp.concatenate([along[:, :span], along[:, span:]], axis=0)
+    a_t[...] = jnp.transpose(stacked).reshape(n * m, jr, lanes)
+    fields[me] = a_t[me]
+    loads[0].wait()
+    pl.semaphore_wait(barrier, n * m - 1)
+
+    to_x, to_y, to_core = m, 2, 1
+    line = [e * m for e in range(0, n, 2)]
+
+    def relay(block, lane, sem, d):
+        send(v.at[block], v.at[block], lane, sem, at(d))
+
+    for i in reversed(range(1, len(line))):
+        relay(me, 0, line_sem.at[i], line[i])
+    relay(me, 0, x_sem.at[0], to_x)
+    relay(me, 0, y_sem.at[0], to_y)
+    for d in far:
+        send(a_t.at[slot(d)], fields.at[me], 1, a_sem, at(d))
+    relay(me, 0, core_sem.at[0, 0], to_core)
+
+    def build(block_g, block_c):
+        hi, lo = split(v[block_g * m + block_c])
+        across = pl.ds(pl.multiple_of(block_c * kc, 128), kc)
+        down = pl.ds(pl.multiple_of(block_g * rows, 16), rows)
+        w_hi[down, across] = hi
+        w_lo[down, across] = lo
+
+    def build_at(d):
+        build(moved(g, g_bits, d // m), moved(c, c_bits, d % m))
+
+    def take_line(i):
+        block = slot(line[i])
+        if i:
+            arrived(v.at[block], line_sem.at[i])
+            relay(block, 0, x_sem.at[i], to_x)
+            relay(block, 0, y_sem.at[i], to_y)
+            relay(block, 0, core_sem.at[0, i], to_core)
+        build_at(line[i])
+
+    def take_x(i):
+        block = slot(line[i] + to_x)
+        arrived(v.at[block], x_sem.at[i])
+        part = v.at[block, pl.ds(0, half)]
+        send(part, part, 0, corner_sem.at[0, i], at(to_y))
+        relay(block, 0, core_sem.at[1, i], to_core)
+        build_at(line[i] + to_x)
+
+    def take_y(i):
+        block = slot(line[i] + to_y)
+        arrived(v.at[block], y_sem.at[i])
+        part = v.at[block, pl.ds(half, half)]
+        send(part, part, 0, corner_sem.at[1, i], at(to_x))
+        relay(block, 0, core_sem.at[2, i], to_core)
+        build_at(line[i] + to_y)
+
+    def take_corner(i):
+        block = slot(line[i] + to_x + to_y)
+        for k in range(2):
+            part = v.at[block, pl.ds(k * half, half)]
+            arrived(part, corner_sem.at[k, i])
+        relay(block, 0, core_sem.at[3, i], to_core)
+        build_at(line[i] + to_x + to_y)
+
+    for i in range(len(line)):
+        take_line(i)
+        take_x(i)
+        take_y(i)
+        if i:
+            take_corner(i - 1)
+
+    loads[3].wait()
+    loads[4].wait()
+    y_col[...] = jnp.transpose(jnp.broadcast_to(yval[...], (128, width)))
+    base = jnp.concatenate(
+        [y_col[pl.ds(pl.multiple_of(h * span + me * jr, 8), jr), 0:1] for h in range(2)], axis=0
+    ) + zval[...]
+    for i in range(m):
+        inverse_sum[i] = 1.0 / (base + x_values[i])
+    take_corner(len(line) - 1)
+
+    for i in range(len(line)):
+        for k, d in enumerate([0, to_x, to_y, to_x + to_y]):
+            arrived(v.at[slot(line[i] + d + to_core)], core_sem.at[k, i])
+            build_at(line[i] + d + to_core)
+
+    low = lax.broadcasted_iota(jnp.int32, (jr, lanes), 1) < rows
+    arrived(fields.at[pl.ds(0, n * m - 1)], a_sem)
+
+    def pair(a, b):
+        return (
+            jnp.where(low, a, pltpu.roll(b, rows, axis=1)),
+            jnp.where(low, pltpu.roll(a, rows, axis=1), b),
+        )
+
+    stack = []
+    for x in range(m):
+        pairs = [pair(fields[2 * t * m + x], fields[(2 * t + 1) * m + x]) for t in range(n // 2)]
+        for h in range(2):
+            stack.append(jnp.concatenate([both[h] for both in pairs], axis=1))
+    modes = product(jnp.concatenate(stack, axis=0), w_hi[...], w_lo[...])
+
+    deep = 2 * jr
+    lines = [modes[x * deep:(x + 1) * deep] for x in range(m)]
+    scaled = []
+    for i in range(m):
+        total = x_vectors[0, i] * lines[0]
+        for x in range(1, m):
+            total = total + x_vectors[x, i] * lines[x]
+        scaled.append(total * inverse_sum[i])
+    turned = []
+    for x in range(m):
+        total = x_vectors[x, 0] * scaled[0]
+        for i in range(1, m):
+            total = total + x_vectors[x, i] * scaled[i]
+        turned.append(total)
+    turned = jnp.concatenate(turned, axis=0)
+    t_hi, t_lo = split(turned)
+    t_both = jnp.concatenate([t_hi, t_lo], axis=0)
+
+    both = dot(t_both, w_hi[...], True)
+    values = both[:m * deep] + (both[m * deep:] + dot(t_hi, w_lo[...], True))
+    for t in range(n // 2):
+        for x in range(m):
+            ends = [values[x * deep + h * jr:x * deep + (h + 1) * jr, t * lanes:(t + 1) * lanes] for h in range(2)]
+            even, odd = pair(*ends)
+            partial[2 * t * m + x] = even
+            partial[(2 * t + 1) * m + x] = odd
+    for d in far:
+        send(partial.at[slot(d)], back.at[me], 2, q_sem, at(d))
+    back[me] = partial[me]
+
+    arrived(back.at[pl.ds(0, n * m - 1)], q_sem)
+    turned_back = jnp.transpose(back[...].reshape(n * m * jr, lanes))
+    lines_back = jnp.concatenate([turned_back[:rows], turned_back[rows:]], axis=1)
+    out[...] = product(lines_back, y_hi[...], y_lo[...], True)
+
+    arrived(v.at[pl.ds(0, n * m - 1)], send_sem.at[0])
+    arrived(fields.at[pl.ds(0, n * m - 1)], send_sem.at[1])
+    arrived(back.at[pl.ds(0, n * m - 1)], send_sem.at[2])
+
+
+def whole_shards(n, m, source, z_vectors, x_vectors, y_vectors, z_values, x_values, y_values):
+    rows, width = source.shape
+    kc = z_vectors.shape[1]
+    jr, lanes, order = width // (2 * n * m), 2 * rows, n * rows
+    vm = pltpu.VMEM
+    dma = pltpu.SemaphoreType.DMA
+    hbm, smem = pl.BlockSpec(memory_space=pl.ANY), pl.BlockSpec(memory_space=pltpu.SMEM)
+    tiles = (n * m, jr, lanes)
+    return pl.pallas_call(
+        functools.partial(whole_kernel, n, m),
+        out_shape=jax.ShapeDtypeStruct((rows, width), f32),
+        in_specs=[hbm] * 5 + [smem] * 2,
+        out_specs=pl.BlockSpec(memory_space=vm),
+        scratch_shapes=[
+            vm((rows, width), f32),
+            vm(y_vectors.shape, f32),
+            vm(y_vectors.shape, bf16),
+            vm(y_vectors.shape, bf16),
+            vm((1, order), f32),
+            vm((1, width), f32),
+            vm((width, 128), f32),
+            vm((m, 2 * jr, order), f32),
+            vm((n * m, rows, kc), f32),
+            vm((order, order), bf16),
+            vm((order, order), bf16),
+            vm(tiles, f32),
+            vm(tiles, f32),
+            vm(tiles, f32),
+            vm(tiles, f32),
+            dma((5,)),
+            dma((3,)),
+            dma,
+            dma,
+            dma((n // 2,)),
+            dma((n // 2,)),
+            dma((n // 2,)),
+            dma((2, n // 2)),
+            dma((4, n // 2)),
+        ],
+        compiler_params=pltpu.CompilerParams(
+            collective_id=0, has_side_effects=True, vmem_limit_bytes=60 * 1024 * 1024
+        ),
+    )(
+        source, z_vectors, y_vectors, z_values.reshape(1, -1), y_values.reshape(1, -1),
+        x_vectors, x_values,
+    )
+
+
+def fits_whole(n, m, source, z_vectors):
+    rows, width = source.shape
+    order = z_vectors.shape[0] * n
+    return (
+        rows == 64 and m == 4 and n <= 8 and n % 2 == 0 and order * order <= 1 << 20
+        and z_vectors.shape[1] % 128 == 0 and width % (16 * n * m) == 0
+    )
+
+
 def solution(mesh):
     placed = (P("gz", "col"), P("gz", "col"), P(), P(), P(), P(), P())
     sizes = (mesh.shape["gz"], mesh.shape["col"])
+
+    def body(source, z_vectors, *rest):
+        chosen = whole_shards if fits_whole(*sizes, source, z_vectors) else shards
+        return chosen(*sizes, source, z_vectors, *rest)
+
     return jax.shard_map(
-        functools.partial(shards, *sizes),
+        body,
         mesh=mesh, in_specs=placed, out_specs=P("gz", "col"), check_vma=False,
     )

time: 29.8 us -> 33.7 us (1.13)
  Pallas kernels: 28 us -> 31.9 us
    pallas_call x1, Pallas kernels: 28 us -> 31.9 us  [whole_shards(): pl.pallas_call(functools.partial(whole_kernel, n, m), out_shape=jax.Shape...]
where the time goes in v1:
time: 33.7 us; the launch traced here: 33.5 us
  Pallas kernels  31.9 us (95%)
  local copies, waits for them, and re-layouts  1.57 us (5%)
    pallas_call x1, Pallas kernels, whole_shards(): pl.pallas_call(functools.partial(whole_kernel, n, m), out_shape=jax.Shape...  31.9 us
    unnamed x1, local copies, waits for them, and re-layouts  1.57 us

profile of v1, /device:TPU:0, one launch (start us, length us, event | category | flops | bytes accessed | tf_op | source)
XLA Modules:
  0.0 33.5 jit_solution(11313589208420792440)
XLA Ops:
  0.0 31.9 %shard_map.73 = f32[64,512]{1,0:T(8,128)} custom-call(f32[64,512]{1,0:T(8,128)} %source.1, f32[64,128]{1,0:T(8,128)} %z_vectors.1, f32[512,512]{1,0:T(8,128)} %y_vectors.1, f32[1,512]{1,0:T(1,128)} %bitcast.2, f32[1,512]{1,0:T(1,128)} %bitcast.3, f32[4,4]{1,0:T(4,128)} %x_vectors.1, f32[4]{0:T(128)} %x_values.1), custom_call_target="tpu_custom_call" | custom-call | tf_op jit(solution)/shard_map/pallas_call | solution.py:572
  31.9 1.6 %copy.9 = f32[64,512]{1,0:T(8,128)} copy(f32[64,512]{1,0:T(8,128)} %shard_map.73) | data formatting | bytes 262144

commit v2 on v1

--- a/solution.py
+++ b/solution.py
@@ -370,11 +370,12 @@
 
 def whole_kernel(
     n, m,
-    source, z_vectors, y_vectors, z_values, y_values, x_vectors, x_values,
+    source, z_vectors, y_vectors, z_values, y_values, x_vectors_in, x_values_in,
     out,
-    src, y_raw, y_hi, y_lo, zval, yval, y_col,
+    src, y_raw, y_hi, y_lo, zval, yval, x_vectors, x_values, y_col,
     inverse_sum, v, w_hi, w_lo, a_t, fields, partial, back,
     load_sem, send_sem, a_sem, q_sem, line_sem, x_sem, y_sem, corner_sem, core_sem,
+    known_sem,
 ):
     g, c = lax.axis_index("gz"), lax.axis_index("col")
     rows, width = src.shape
@@ -404,16 +405,34 @@
     loads = [
         pltpu.make_async_copy(a, b, load_sem.at[i])
         for i, (a, b) in enumerate(
-            [(z_vectors, v.at[me]), (y_vectors, y_raw), (source, src), (z_values, zval), (y_values, yval)]
+            [(z_vectors, v.at[me]), (y_vectors, y_raw), (source, src), (z_values, zval), (y_values, yval),
+             (x_vectors_in, x_vectors), (x_values_in, x_values)]
         )
     ]
+    to_x, to_y, to_core = m, 2, 1
+    line = [e * m for e in range(0, n, 2)]
+    barrier = pltpu.get_barrier_semaphore()
+    for d in line[:0:-1] + [to_x, to_y, to_core]:
+        pl.semaphore_signal(barrier, inc=1, device_id=at(d), device_id_type=MESH)
     for copy in loads:
         copy.start()
-    barrier = pltpu.get_barrier_semaphore()
     far = sorted(range(1, n * m), key=lambda d: -bin(d).count("1") - (d // m // 2))
-    for d in far:
-        pl.semaphore_signal(barrier, inc=1, device_id=at(d), device_id_type=MESH)
-
+    def relay(block, lane, sem, d):
+        send(v.at[block], v.at[block], lane, sem, at(d))
+
+    def tell(k):
+        pl.semaphore_signal(
+            known_sem.at[k], inc=1, device_id=at([to_x, to_y, to_core][k]), device_id_type=MESH
+        )
+
+    pl.semaphore_wait(barrier, len(line) + 2)
+    tell(0)
+    loads[0].wait()
+    for i in reversed(range(1, len(line))):
+        relay(me, 0, line_sem.at[i], line[i])
+    relay(me, 0, x_sem.at[0], to_x)
+    relay(me, 0, y_sem.at[0], to_y)
+    relay(me, 0, core_sem.at[0, 0], to_core)
     loads[1].wait()
     hi, lo = split(y_raw[...])
     y_hi[...] = hi
@@ -423,22 +442,12 @@
     stacked = jnp.concatenate([along[:, :span], along[:, span:]], axis=0)
     a_t[...] = jnp.transpose(stacked).reshape(n * m, jr, lanes)
     fields[me] = a_t[me]
-    loads[0].wait()
-    pl.semaphore_wait(barrier, n * m - 1)
-
-    to_x, to_y, to_core = m, 2, 1
-    line = [e * m for e in range(0, n, 2)]
-
-    def relay(block, lane, sem, d):
-        send(v.at[block], v.at[block], lane, sem, at(d))
-
-    for i in reversed(range(1, len(line))):
-        relay(me, 0, line_sem.at[i], line[i])
-    relay(me, 0, x_sem.at[0], to_x)
-    relay(me, 0, y_sem.at[0], to_y)
+    for k, d in enumerate([to_x, to_y, to_core]):
+        pl.semaphore_wait(known_sem.at[k], 1)
+        if d != to_core:
+            tell(k + 1)
     for d in far:
         send(a_t.at[slot(d)], fields.at[me], 1, a_sem, at(d))
-    relay(me, 0, core_sem.at[0, 0], to_core)
 
     def build(block_g, block_c):
         hi, lo = split(v[block_g * m + block_c])
@@ -450,30 +459,26 @@
     def build_at(d):
         build(moved(g, g_bits, d // m), moved(c, c_bits, d % m))
 
-    def take_line(i):
+    def forward_line(i):
         block = slot(line[i])
-        if i:
-            arrived(v.at[block], line_sem.at[i])
-            relay(block, 0, x_sem.at[i], to_x)
-            relay(block, 0, y_sem.at[i], to_y)
-            relay(block, 0, core_sem.at[0, i], to_core)
-        build_at(line[i])
-
-    def take_x(i):
+        arrived(v.at[block], line_sem.at[i])
+        relay(block, 0, x_sem.at[i], to_x)
+        relay(block, 0, y_sem.at[i], to_y)
+        relay(block, 0, core_sem.at[0, i], to_core)
+
+    def forward_x(i):
         block = slot(line[i] + to_x)
         arrived(v.at[block], x_sem.at[i])
         part = v.at[block, pl.ds(0, half)]
         send(part, part, 0, corner_sem.at[0, i], at(to_y))
         relay(block, 0, core_sem.at[1, i], to_core)
-        build_at(line[i] + to_x)
-
-    def take_y(i):
+
+    def forward_y(i):
         block = slot(line[i] + to_y)
         arrived(v.at[block], y_sem.at[i])
         part = v.at[block, pl.ds(half, half)]
         send(part, part, 0, corner_sem.at[1, i], at(to_x))
         relay(block, 0, core_sem.at[2, i], to_core)
-        build_at(line[i] + to_y)
 
     def take_corner(i):
         block = slot(line[i] + to_x + to_y)
@@ -483,22 +488,26 @@
         relay(block, 0, core_sem.at[3, i], to_core)
         build_at(line[i] + to_x + to_y)
 
+    for i in range(1, len(line)):
+        forward_line(i)
     for i in range(len(line)):
-        take_line(i)
-        take_x(i)
-        take_y(i)
-        if i:
-            take_corner(i - 1)
+        forward_x(i)
+        forward_y(i)
+    for i in range(len(line)):
+        for d in (0, to_x, to_y):
+            build_at(line[i] + d)
 
     loads[3].wait()
-    loads[4].wait()
+    for copy in loads[4:]:
+        copy.wait()
     y_col[...] = jnp.transpose(jnp.broadcast_to(yval[...], (128, width)))
     base = jnp.concatenate(
         [y_col[pl.ds(pl.multiple_of(h * span + me * jr, 8), jr), 0:1] for h in range(2)], axis=0
     ) + zval[...]
     for i in range(m):
         inverse_sum[i] = 1.0 / (base + x_values[i])
-    take_corner(len(line) - 1)
+    for i in range(len(line)):
+        take_corner(i)
 
     for i in range(len(line)):
         for k, d in enumerate([0, to_x, to_y, to_x + to_y]):
@@ -567,12 +576,12 @@
     jr, lanes, order = width // (2 * n * m), 2 * rows, n * rows
     vm = pltpu.VMEM
     dma = pltpu.SemaphoreType.DMA
-    hbm, smem = pl.BlockSpec(memory_space=pl.ANY), pl.BlockSpec(memory_space=pltpu.SMEM)
+    hbm = pl.BlockSpec(memory_space=pl.ANY)
     tiles = (n * m, jr, lanes)
     return pl.pallas_call(
         functools.partial(whole_kernel, n, m),
         out_shape=jax.ShapeDtypeStruct((rows, width), f32),
-        in_specs=[hbm] * 5 + [smem] * 2,
+        in_specs=[hbm] * 7,
         out_specs=pl.BlockSpec(memory_space=vm),
         scratch_shapes=[
             vm((rows, width), f32),
@@ -581,6 +590,8 @@
             vm(y_vectors.shape, bf16),
             vm((1, order), f32),
             vm((1, width), f32),
+            pltpu.SMEM(x_vectors.shape, f32),
+            pltpu.SMEM(x_values.shape, f32),
             vm((width, 128), f32),
             vm((m, 2 * jr, order), f32),
             vm((n * m, rows, kc), f32),
@@ -590,7 +601,7 @@
             vm(tiles, f32),
             vm(tiles, f32),
             vm(tiles, f32),
-            dma((5,)),
+            dma((7,)),
             dma((3,)),
             dma,
             dma,
@@ -599,6 +610,7 @@
             dma((n // 2,)),
             dma((2, n // 2)),
             dma((4, n // 2)),
+            pltpu.SemaphoreType.REGULAR((3,)),
         ],
         compiler_params=pltpu.CompilerParams(
             collective_id=0, has_side_effects=True, vmem_limit_bytes=60 * 1024 * 1024

time: 33.7 us -> 26.8 us (0.80)
  Pallas kernels: 31.9 us -> 25.1 us
    pallas_call x1, Pallas kernels: 31.9 us -> 25.1 us  [whole_shards(): pl.pallas_call(functools.partial(whole_kernel, n, m), out_shape=jax.Shape...]
where the time goes in v2:
time: 26.8 us; the launch traced here: 26.7 us
  Pallas kernels  25.1 us (94%)
  local copies, waits for them, and re-layouts  1.57 us (6%)
    pallas_call x1, Pallas kernels, whole_shards(): pl.pallas_call(functools.partial(whole_kernel, n, m), out_shape=jax.Shape...  25.1 us
    unnamed x1, local copies, waits for them, and re-layouts  1.57 us

profile of v2, /device:TPU:0, one launch (start us, length us, event | category | flops | bytes accessed | tf_op | source)
XLA Modules:
  0.0 26.7 jit_solution(12042617460958390765)
XLA Ops:
  0.0 25.1 %shard_map.73 = f32[64,512]{1,0:T(8,128)} custom-call(f32[64,512]{1,0:T(8,128)} %source.1, f32[64,128]{1,0:T(8,128)} %z_vectors.1, f32[512,512]{1,0:T(8,128)} %y_vectors.1, f32[1,512]{1,0:T(1,128)} %bitcast.2, f32[1,512]{1,0:T(1,128)} %bitcast.3, f32[4,4]{1,0:T(4,128)} %x_vectors_in.1, f32[4]{0:T(128)} %x_values_in.1), custom_call_target="tpu_custom_call" | custom-call | tf_op jit(solution)/shard_map/pallas_call | solution.py:581
  25.1 1.6 %copy.9 = f32[64,512]{1,0:T(8,128)} copy(f32[64,512]{1,0:T(8,128)} %shard_map.73) | data formatting | bytes 262144
